TPU v7x, 256 devices: a whole 4x4x8 slice. The times are simulated.
256 devices in a mesh: rel: 8 (over x, z_lo), ent: 32 (over z_hi, y, core).
Axes of the slice: x: 4, y: 4, z: 8 (z_hi: 4, z_lo: 2; z = z_hi * 2 + z_lo), core: 2. Of those that a mesh axis runs over, the one named last changes fastest.
Arguments:
- state: bfloat16 [8192, 1024], P('ent', 'rel'), may hold values from -4 to 4
- rel_weight: bfloat16 [24, 1024, 1024], P('rel', 'ent'), may hold values from -0.0390625 to 0.0390625
- gate_weight: bfloat16 [1024, 1024], P(None, 'rel'), may hold values from -0.1875 to 0.1875
- gate_bias: float32 [1024], P('rel'), may hold values from -4 to 4
- update_bias: float32 [1024], P('rel'), may hold values from -3 to 3
- tile_values: bfloat16 [8, 512, 128, 128], P('rel', 'ent'), may hold values from 0 to 0.119628906
- tile_index: int32 [8, 3, 512], P('rel', None, 'ent'), may hold values from 0 to 63, as said below
- tile_count: int32 [8, 32], P('rel', 'ent'), may hold values from 1 to 16, as said below
Outputs:
- new_state: bfloat16 [8192, 1024], P('ent', 'rel')
Inputs may be any that keep to these rules, and one draw needn't show every extreme that they name: `tile_index`: row 0 names a source tile of the whole graph, row 1 a destination tile of the partition that owns the slot (below 2), row 2 a relation within the group (below 3). `tile_count`: slots of a partition at or past its count are padding; in every group some partition fills all 16 slots.
All inputs are finite; a program needn't handle non-finite values.
Results may differ from a plain program's by a relative error of at most 0.0065.
Values may be sent and summed in bfloat16 or wider, within the bound.
A program may use at most 128 MiB of HBM per device.

v0:
```python
import jax
import jax.numpy as jnp
from jax import lax
from jax.sharding import PartitionSpec as P


def copy_for_each(x, axis):
    count = lax.axis_size(axis)
    return lax.all_to_all(jnp.broadcast_to(x[None], (count, *x.shape)), axis, 0, 0, tiled=True)


def laid_out(blocks, dim):
    dims = list(blocks.shape[1:])
    dims[dim] *= blocks.shape[0]
    return jnp.moveaxis(blocks, 0, dim).reshape(dims)


def gather_directly(x, axis, dim):
    blocks = copy_for_each(x, axis)
    return laid_out(blocks, dim)


def in_blocks(x, dim, count):
    dims = x.shape
    blocks = x.reshape(*dims[:dim], count, dims[dim] // count, *dims[dim + 1 :])
    return jnp.moveaxis(blocks, dim, 0)


def summed_on_arrival(x, axis, dim):
    count = lax.axis_size(axis)
    blocks = lax.all_to_all(in_blocks(x, dim, count), axis, 0, 0, tiled=True)
    return jnp.sum(blocks.astype(jnp.float32), axis=0)


def collect(gathered, tile_values, tile_index, tile_count, rel_dev, per_tile):
    tile_rows = tile_values.shape[-1]
    features = gathered.shape[1]
    stacked = gathered.reshape(-1, tile_rows, features)
    listing = tile_index[0]
    values = tile_values[0]
    live_total = tile_count[0, 0]
    classes = per_tile * rel_dev
    slab_rows = min(8, values.shape[0])
    class_ids = jnp.arange(classes, dtype=jnp.int32)

    def accumulate(turn_num, summed):
        first_slot = turn_num * slab_rows
        slab_values = lax.dynamic_slice_in_dim(values, first_slot, slab_rows, 0)
        picked = lax.dynamic_slice_in_dim(listing, first_slot, slab_rows, 1)
        sources = stacked[picked[0]]
        product = jnp.einsum(
            "sij,sjh->sih", slab_values, sources, preferred_element_type=jnp.float32
        )
        slot_ids = first_slot + jnp.arange(slab_rows, dtype=jnp.int32)
        live_mask = (slot_ids < live_total).astype(jnp.float32)
        target = picked[1] * rel_dev + picked[2]
        select = (target[:, None] == class_ids[None, :]).astype(jnp.float32) * live_mask[:, None]
        return summed + jnp.einsum("sk,sih->kih", select, product, precision=lax.Precision.HIGHEST)

    initial = jnp.zeros((classes, tile_rows, features), jnp.float32)
    turn_total = (live_total + slab_rows - 1) // slab_rows
    return lax.fori_loop(0, turn_total, accumulate, initial)


def shards(
    state, rel_weight, gate_weight, gate_bias, update_bias, tile_values, tile_index, tile_count
):
    rel_dev = rel_weight.shape[0]
    ent_dev = state.shape[0]
    tile_rows = tile_values.shape[-1]
    per_tile = ent_dev // tile_rows
    features = rel_weight.shape[2]
    relation_full = lax.all_gather(rel_weight, "ent", axis=1, tiled=True)
    columns = state
    own_rows = gather_directly(columns, "rel", 1)
    gathered = lax.all_gather(own_rows, "ent", axis=0, tiled=True)
    summed = collect(gathered, tile_values, tile_index, tile_count, rel_dev, per_tile)
    aggregate = summed.astype(jnp.bfloat16).reshape(per_tile, rel_dev, tile_rows, features)
    group_terms = jnp.einsum(
        "drih,rhk->dik", aggregate, relation_full, preferred_element_type=jnp.float32
    )
    message = summed_on_arrival(
        group_terms.reshape(ent_dev, features).astype(jnp.bfloat16), "rel", 1
    )
    gate_open = jax.nn.sigmoid(
        jnp.dot(own_rows, gate_weight, preferred_element_type=jnp.float32) + gate_bias
    )
    update = jnp.tanh(message + update_bias)
    columns = ((1.0 - gate_open) * columns.astype(jnp.float32) + gate_open * update).astype(
        jnp.bfloat16
    )
    return columns


def solution(mesh):
    in_specs = (
        P("ent", "rel"),
        P("rel", "ent", None),
        P(None, "rel"),
        P("rel"),
        P("rel"),
        P("rel", "ent", None, None),
        P("rel", None, "ent"),
        P("rel", "ent"),
    )
    out_specs = P("ent", "rel")
    return jax.shard_map(shards, mesh=mesh, in_specs=in_specs, out_specs=out_specs, check_vma=False)
```

profile of v0, /device:TPU:1, one launch (start us, length us, event | category | flops | bytes accessed | tf_op | source)
XLA Modules:
  0.0 249.2 jit_solution(5993001799591295696)
XLA Ops:
  6.5 0.0 copy-start
  6.5 0.0 all-gather.3.cloned.1.call-start
  6.5 0.9 broadcast_in_dim.4
  7.5 15.3 %all_to_all.10 = bf16[8,256,128]{2,1,0:T(8,128)(2,1)S(1)} all-to-all(bf16[8,256,128]{2,1,0:T(8,128)(2,1)S(1)} %broadcast_in_dim.4), channel_id=1, replica_groups=mesh['rel'=8,'ent'=32] {'rel'}, dimensions={0} | all-to-all | bytes 1048576 | tf_op jit(solution)/shard_map/all_to_all | solution.py:9
  22.8 1.0 copy.19
  23.8 0.0 all-gather.3.cloned.1.call-update
  23.8 0.0 all-gather.5.cloned.1.call-start
  23.9 0.7 all-gather.5.cloned.1.call-update
  25.2 0.7 copy.36
  25.9 127.5 %all-gather.3.cloned.1.call-done = bf16[8192,1024]{0,1:T(8,128)(2,1)} async-done(((bf16[256,1024]{0,1:T(8,128)(2,1)}), bf16[8192,1024]{0,1:T(8,128)(2,1)}) %all-gather.3.cloned.1.call-update) | async-done | bytes 16777232 | tf_op jit(solution)/shard_map/all_gather | solution.py:76
  153.5 22.3 %copy.24 = bf16[8192,1024]{1,0:T(8,128)(2,1)} copy(bf16[8192,1024]{0,1:T(8,128)(2,1)} %all-gather.3.cloned.1.call-done) | data formatting | bytes 33554432
  175.8 0.0 copy-start.1
  175.8 2.5 broadcast_in_dim.5
  178.3 0.0 copy-done.1
  178.3 32.7 %while.11 = (s32[]{:T(128)}, f32[6,128,1024]{2,0,1:T(8,128)}, s32[]{:T(128)}, s32[3,16]{1,0:T(4,128)S(1)}, s32[]{:T(128)}, /*index=5*/bf16[16,128,128]{2,1,0:T(8...) while((s32[]{:T(128)}, f32[6,128,1024]{2,0,1:T(8,128)}, ...), condition=%wide.region_1.2_spmd.clone, body=%wide.region_0.1_spmd.clone.sunk | while | flops 344720544 | bytes 21238444 | solution.py:62
  178.3 0.1 constant_dynamic-slice_fusion.2
  178.4 6.5 %gather_fusion = bf16[8,128,1024]{2,1,0:T(8,128)(2,1)S(1)} fusion(bf16[64,128,1024]{2,1,0:T(8,128)(2,1)} %get-tuple-element.159, s32[1024]{0:T(1024)S(1)} %pad_clamp_fusion.2), kind=kCustom, calls=%fused_computation.clone.clone.1 | custom fusion | bytes 4194336 | tf_op jit(solution)/shard_map/while/body/gather | solution.py:50
  184.8 0.7 fusion.40
  185.5 0.7 compare_convert_fusion.2
  186.2 8.3 %fusion.41 = f32[6,128,1024]{2,0,1:T(8,128)} fusion(f32[6,128,1024]{2,0,1:T(8,128)} %get-tuple-element.143, f32[8,128,1024]{2,1,0:T(8,128)S(1)} %fusion.40, f32[8]{0:T(128)S(1)} %compare_convert_fusion.2, s32[8]{0:T(128)S(1)} %add_bitcast_fusion.2), kind=kOutput, calls=%fused_computation.4.clone.1 | convolution fusion | flops 76284000 | bytes 10485824 | tf_op jit(solution)/shard_map/while/body/sk,sih->kih/dot_general | solution.py:58
  194.5 0.1 constant_dynamic-slice_fusion.2
  194.6 6.7 %gather_fusion = bf16[8,128,1024]{2,1,0:T(8,128)(2,1)S(1)} fusion(bf16[64,128,1024]{2,1,0:T(8,128)(2,1)} %get-tuple-element.159, s32[1024]{0:T(1024)S(1)} %pad_clamp_fusion.2), kind=kCustom, calls=%fused_computation.clone.clone.1 | custom fusion | bytes 4194336 | tf_op jit(solution)/shard_map/while/body/gather | solution.py:50
  201.3 0.7 fusion.40
  202.0 0.7 compare_convert_fusion.2
  202.6 8.3 %fusion.41 = f32[6,128,1024]{2,0,1:T(8,128)} fusion(f32[6,128,1024]{2,0,1:T(8,128)} %get-tuple-element.143, f32[8,128,1024]{2,1,0:T(8,128)S(1)} %fusion.40, f32[8]{0:T(128)S(1)} %compare_convert_fusion.2, s32[8]{0:T(128)S(1)} %add_bitcast_fusion.2), kind=kOutput, calls=%fused_computation.4.clone.1 | convolution fusion | flops 76284000 | bytes 10485824 | tf_op jit(solution)/shard_map/while/body/sk,sih->kih/dot_general | solution.py:58
  210.9 3.9 %copy.34 = bf16[6,128,1024]{2,1,0:T(8,128)(2,1)S(1)} copy(f32[6,128,1024]{2,0,1:T(8,128)} %get-tuple-element.48) | data formatting | bytes 4718592 | tf_op jit(solution)/shard_map/while | solution.py:62
  214.9 0.2 copy.22
  215.0 8.4 %all-gather.5.cloned.1.call-done = bf16[3,1024,1024]{2,1,0:T(8,128)(2,1)} async-done(((bf16[3,32,1024]{2,1,0:T(8,128)(2,1)}), bf16[3,1024,1024]{2,1,0:T(8,128)(2,1)}) %all-gather.5.cloned.1.call-update) | async-done | bytes 6291472 | tf_op jit(solution)/shard_map/all_gather | solution.py:73
  223.4 0.0 copy-start.2
  223.4 0.0 copy-start.3
  223.4 0.0 copy-start.4
  223.4 0.0 copy-start.5
  223.4 4.6 %fusion.18 = bf16[32,8,8,128]{3,2,1,0:T(8,128)(2,1)S(1)} fusion(bf16[256,1024,3]{1,0,2:T(8,128)(2,1)S(1)} %bitcast.58, bf16[3,1024,1024]{2,1,0:T(8,128)(2,1)} %all-gather.5.cloned.1.call-done), kind=kOutput, calls=%fused_computation.24 | convolution fusion | flops 1610874880 | bytes 8388608 | tf_op jit(solution)/shard_map/drih,rhk->dik/dot_general | solution.py:79
  228.1 0.1 copy.35
  228.2 13.1 %all_to_all.11 = bf16[8,256,128]{2,1,0:T(8,128)(2,1)S(1)} all-to-all(bf16[8,256,128]{2,1,0:T(8,128)(2,1)S(1)} %bitcast.57), channel_id=1, replica_groups=mesh['rel'=8,'ent'=32] {'rel'}, dimensions={0} | all-to-all | bytes 1048576 | tf_op jit(solution)/shard_map/all_to_all | solution.py:31
  241.3 0.1 convert_reduce_fusion
  241.3 0.0 copy-done
  241.4 0.0 copy-done.2
  241.4 0.0 copy-done.3
  241.4 0.0 copy-done.4
  241.4 0.0 copy-done.5
  241.4 1.0 add_convert_fusion
  (6 shorter events, 0.0 us)
Async XLA Ops:
  6.5 234.8 %copy-start = (bf16[1024,128]{1,0:T(8,128)(2,1)S(1)}, bf16[1024,128]{1,0:T(8,128)(2,1)}, u32[]{:S(2)}) copy-start(bf16[1024,128]{1,0:T(8,128)(2,1)} %param.12) | copy-start | bytes 786436
  6.5 146.9 %all-gather.3.cloned.1.call-start = ((), (), s32[]{:S(2)}) async-start(), calls=%async_computation.2 | async-start | bytes 17301504 | tf_op jit(solution)/shard_map/all_gather | solution.py:76
  23.8 199.6 %all-gather.5.cloned.1.call-start = ((), (), s32[]{:S(2)}) async-start(), calls=%async_computation.3 | async-start | bytes 6488064 | tf_op jit(solution)/shard_map/all_gather | solution.py:73
  175.8 2.5 copy-start.1
  223.4 17.9 %copy-start.2 = (bf16[8,256,128]{1,2,0:T(8,128)(2,1)S(1)}, bf16[8,256,128]{1,2,0:T(8,128)(2,1)}, u32[]{:S(2)}) copy-start(bf16[8,256,128]{1,2,0:T(8,128)(2,1)} %copy.19) | copy-start | bytes 1572868
  223.4 18.0 %copy-start.3 = (bf16[256,128]{1,0:T(8,128)(2,1)S(1)}, bf16[256,128]{1,0:T(8,128)(2,1)}, u32[]{:S(2)}) copy-start(bf16[256,128]{1,0:T(8,128)(2,1)} %param.10) | copy-start | bytes 196612
  223.4 18.0 %copy-start.4 = (f32[128]{0:T(128)S(1)}, f32[128]{0:T(128)}, u32[]{:S(2)}) copy-start(f32[128]{0:T(128)} %param.14) | copy-start | bytes 1540
  223.4 18.0 %copy-start.5 = (f32[128]{0:T(128)S(1)}, f32[128]{0:T(128)}, u32[]{:S(2)}) copy-start(f32[128]{0:T(128)} %param.13) | copy-start | bytes 1540
Sparse Core Ops, SparseCore 0:
  23.9 129.4 all-gather.2
  156.1 67.3 all-gather.4
where the time goes:
time: 250 us; the launch traced here: 249 us
  waiting for transfers between devices  137 us (55%)
  local copies, waits for them, and re-layouts  45 us (18%)
  blocking collectives  28.4 us (11%)
  matrix products  23.6 us (9%)
  between operations  14.1 us (6%)
    all_gather x1, waiting for transfers between devices, shards(): gathered = lax.all_gather(own_rows, 'ent', axis=0, tiled=True)  128 us
    unnamed x14, local copies, waits for them, and re-layouts  23 us
    dot_general x2, matrix products, accumulate(): jnp.einsum('sk,sih->kih', select, product, precision=lax.Precision.HIGHEST)  16.6 us
    all_to_all x1, blocking collectives, copy_for_each(): lax.all_to_all(jnp.broadcast_to(x[None], (count, *x.shape)), axis, 0, 0,...  15.3 us
    gather x2, local copies, waits for them, and re-layouts, accumulate(): sources = stacked[picked[0]]  13.1 us
    all_to_all x1, blocking collectives, summed_on_arrival(): blocks = lax.all_to_all(in_blocks(x, dim, count), axis, 0, 0, tiled=True)  13.1 us
    all_gather x1, waiting for transfers between devices, shards(): relation_full = lax.all_gather(rel_weight, 'ent', axis=1, tiled=True)  8.39 us
  transfers between devices with their start and end apart: 2, of which 2 were waited for; matrix products, arithmetic and copies ran while one was open for 25% of the time, Pallas kernels for 0%

commit v1 on v0

v1 whole, which is shorter than its diff:
```python
import jax
import jax.numpy as jnp
from jax import lax
from jax.experimental import pallas as pl
from jax.experimental.pallas import tpu as pltpu

MESH = pl.DeviceIdType.MESH
BF = jnp.bfloat16
F32 = jnp.float32


class Sems:
    def __init__(self):
        self.total = 0

    def take(self, count):
        first = self.total
        self.total += count
        return first


S = Sems()
TVP, TVM, TVR = S.take(2), S.take(2), S.take(2)
MET = S.take(3)
SY, SYR = S.take(2), S.take(2)
SZP, SZM = S.take(4), S.take(4)
SD = S.take(8)
GP, GM, GR = S.take(2), S.take(2), S.take(2)
WZP, WZM, WZR0, WZR1 = S.take(3), S.take(3), S.take(3), S.take(3)
WX = S.take(9)
WYP, WYM, WYR0, WYR1 = S.take(12), S.take(12), S.take(12), S.take(12)
WD = S.take(16)
PT = S.take(8)


def kernel(
    meta_in, state_in, relw_in, tv_in, gw_ref, gb_ref, ub_ref, out_ref,
    tvb, metav, metas, sb, rb, wz, wb, lhs, rhs, ab, pb, qb, ssem, rsem, lsem,
):
    rel = lax.axis_index("rel")
    ent = lax.axis_index("ent")
    x, zl = lax.div(rel, 2), lax.rem(rel, 2)
    zh, y, c = lax.div(ent, 8), lax.rem(lax.div(ent, 2), 4), lax.rem(ent, 2)
    z = zh * 2 + zl

    def turn(v, step, count):
        return lax.rem(v + (step + count) % count, count)

    def at(x_=None, y_=None, z_=None, c_=None):
        xx = x if x_ is None else x_
        yy = y if y_ is None else y_
        zz = z if z_ is None else z_
        cc = c if c_ is None else c_
        return (xx * 2 + lax.rem(zz, 2), lax.div(zz, 2) * 8 + yy * 2 + cc)

    xp, xm, x2 = turn(x, 1, 4), turn(x, -1, 4), turn(x, 2, 4)
    yp, ym, y2 = turn(y, 1, 4), turn(y, -1, 4), turn(y, 2, 4)
    hp, hm, h2 = turn(zh, 1, 4), turn(zh, -1, 4), turn(zh, 2, 4)
    zo = zh * 2 + (1 - zl)
    dxp, dxm, dx2 = at(x_=xp), at(x_=xm), at(x_=x2)
    dyp, dym = at(y_=yp), at(y_=ym)
    dzp, dzm = at(z_=turn(z, 1, 8)), at(z_=turn(z, -1, 8))
    dhp, dhm = at(z_=hp * 2 + zl), at(z_=hm * 2 + zl)
    dco = at(c_=1 - c)
    peers = [dxp, dxm, dx2, dyp, dym, dzp, dzm, dhp, dhm, dco]
    peers += [at(x_=v, z_=zo) for v in (xp, xm, x2)]

    pending = []

    def copy(i, src, dst, dev):
        return pltpu.make_async_remote_copy(
            src_ref=src, dst_ref=dst, send_sem=ssem.at[i], recv_sem=rsem.at[i],
            device_id=dev, device_id_type=MESH,
        )

    def send(i, src, dst, dev):
        d = copy(i, src, dst, dev)
        d.start()
        pending.append(d)

    def got(i, ref):
        copy(i, ref, ref, dco).wait_recv()

    yc = y * 2 + c
    own_t = ((zh * 2 + c) * 4 + y) * 2
    row0 = (zh * 2 + c) * 8

    local = [
        pltpu.make_async_copy(relw_in, wz.at[zh], lsem.at[0]),
        pltpu.make_async_copy(state_in, sb.at[zl, pl.ds(own_t, 2)], lsem.at[1]),
        pltpu.make_async_copy(meta_in, metav.at[x], lsem.at[2]),
        pltpu.make_async_copy(tv_in, tvb.at[x], lsem.at[3]),
    ]
    for d in local:
        d.start()
    barrier = pltpu.get_barrier_semaphore()
    for dev in peers:
        pl.semaphore_signal(barrier, inc=1, device_id=dev, device_id_type=MESH)
    for d in local:
        d.wait()
    pl.semaphore_wait(barrier, len(peers))

    for r in range(3):
        send(WZP + r, wz.at[zh, r], wz.at[zh, r], dhp)
        send(WZM + r, wz.at[zh, r], wz.at[zh, r], dhm)
    mine = sb.at[zl, pl.ds(own_t, 2)]
    send(SY, mine, mine, dyp)
    send(SY + 1, mine, mine, dym)
    for k, dev in enumerate((dxp, dxm, dx2)):
        send(MET + k, metav.at[x], metav.at[x], dev)

    def weight_row(slot, r):
        d = lax.rem(slot - x + 4, 4)

        @pl.when(d != 0)
        def _():
            copy(
                WX + (d - 1) * 3 + r, wz.at[slot, r], wb.at[x, r, yc], at(x_=slot)
            ).start()

    for r in range(3):
        weight_row(zh, r)

    def tv_half(x_, h):
        return tvb.at[x_, pl.ds(h * 8, 8)]

    send(TVP, tv_half(x, 0), tv_half(x, 0), dxp)
    send(TVM + 1, tv_half(x, 1), tv_half(x, 1), dxm)

    def piece(y_, first, count):
        return sb.at[zl, pl.ds(row0 + y_ * 2 + first, count)]

    got(SY, piece(ym, 0, 2))
    send(SYR, piece(ym, 0, 1), piece(ym, 0, 1), dyp)
    got(SY + 1, piece(yp, 0, 2))
    send(SYR + 1, piece(yp, 1, 1), piece(yp, 1, 1), dym)

    for r in range(3):
        got(WZP + r, wz.at[hm, r])
        half = wz.at[hm, r, pl.ds(0, 16)]
        send(WZR0 + r, half, half, dhp)
        got(WZM + r, wz.at[hp, r])
        half = wz.at[hp, r, pl.ds(16, 16)]
        send(WZR1 + r, half, half, dhm)
        weight_row(hm, r)
        weight_row(hp, r)

    got(SYR, piece(y2, 0, 1))
    got(SYR + 1, piece(y2, 1, 1))

    def chunk(step, cc, first=0, count=8):
        zz = turn(z, step, 8)
        return sb.at[lax.rem(zz, 2), pl.ds((lax.div(zz, 2) * 2 + cc) * 8 + first, count)]

    def share(k, step):
        send(SD + k, chunk(step, c), chunk(step, c), dco)

    send(SZP, chunk(0, c), chunk(0, c), dzp)
    send(SZM, chunk(0, c), chunk(0, c), dzm)
    share(0, 0)

    for r in range(3):
        got(WZR0 + r, wz.at[h2, r, pl.ds(0, 16)])
        got(WZR1 + r, wz.at[h2, r, pl.ds(16, 16)])
        weight_row(h2, r)

    def block(d, r, y_, cc=None):
        return wb.at[turn(x, -d, 4), r, y_ * 2 + (c if cc is None else cc)]

    def half_block(d, r, y_, h):
        return wb.at[turn(x, -d, 4), r, y_ * 2 + c, pl.ds(h * 16, 16)]

    def whole_block(d, y_, cc=None):
        return wb.at[turn(x, -d, 4), :, y_ * 2 + (c if cc is None else cc)]

    for r in range(3):
        send(WYP + r, wz.at[x, r], block(0, r, y), dyp)
        send(WYM + r, wz.at[x, r], block(0, r, y), dym)
    send(WD, wz.at[x], whole_block(0, y), dco)
    wb[x, :, yc] = wz[x]

    def weights_out(d):
        for r in range(3):
            got(WX + (d - 1) * 3 + r, block(d, r, y))
            send(WYP + d * 3 + r, block(d, r, y), block(d, r, y), dyp)
            send(WYM + d * 3 + r, block(d, r, y), block(d, r, y), dym)
        send(WD + d, whole_block(d, y), whole_block(d, y), dco)

    def weights_on(d):
        for r in range(3):
            got(WYP + d * 3 + r, block(d, r, ym))
            send(WYR0 + d * 3 + r, half_block(d, r, ym, 0), half_block(d, r, ym, 0), dyp)
            got(WYM + d * 3 + r, block(d, r, yp))
            send(WYR1 + d * 3 + r, half_block(d, r, yp, 1), half_block(d, r, yp, 1), dym)
        send(WD + 4 + d, whole_block(d, ym), whole_block(d, ym), dco)
        send(WD + 8 + d, whole_block(d, yp), whole_block(d, yp), dco)

    def weights_end(d):
        for r in range(3):
            got(WYR0 + d * 3 + r, half_block(d, r, y2, 0))
            got(WYR1 + d * 3 + r, half_block(d, r, y2, 1))
        send(WD + 12 + d, whole_block(d, y2), whole_block(d, y2), dco)

    def state_on(k):
        got(SZP + k - 1, chunk(-k, c))
        got(SZM + k - 1, chunk(k, c))
        if k < 3:
            send(SZP + k, chunk(-k, c), chunk(-k, c), dzp)
            send(SZM + k, chunk(k, c), chunk(k, c), dzm)
        else:
            send(SZP + k, chunk(-k, c, 0, 4), chunk(-k, c, 0, 4), dzp)
            send(SZM + k, chunk(k, c, 4, 4), chunk(k, c, 4, 4), dzm)
        share(2 * k - 1, -k)
        share(2 * k, k)

    weights_out(1)
    weights_out(3)
    state_on(1)
    for q in range(2):
        pair = sb.at[q, pl.ds(own_t, 2)]
        send(GP + q, pair, rb.at[x, q], dxp)
        send(GM + q, pair, rb.at[x, q], dxm)
    weights_out(2)
    send(TVP + 1, tv_half(x, 1), tv_half(x, 1), dxp)
    send(TVM, tv_half(x, 0), tv_half(x, 0), dxm)
    weights_on(0)
    state_on(2)
    got(TVP, tv_half(xm, 0))
    send(TVR, tv_half(xm, 0), tv_half(xm, 0), dxp)
    got(TVM + 1, tv_half(xp, 1))
    send(TVR + 1, tv_half(xp, 1), tv_half(xp, 1), dxm)
    weights_on(1)
    state_on(3)
    weights_on(3)
    weights_end(0)
    for q in range(2):
        got(GP + q, rb.at[xm, q])
        got(GM + q, rb.at[xp, q])
    send(GR, rb.at[xm, 0], rb.at[xm, 0], dxp)
    send(GR + 1, rb.at[xp, 1], rb.at[xp, 1], dxm)
    got(SZP + 3, chunk(4, c, 0, 4))
    got(SZM + 3, chunk(4, c, 4, 4))
    share(7, 4)
    weights_on(2)
    for k, v in enumerate((xm, xp, x2)):
        got(MET + k, metav.at[v])
    listing = pltpu.make_async_copy(metav, metas, lsem.at[4])
    listing.start()
    got(TVP + 1, tv_half(xm, 1))
    got(TVM, tv_half(xp, 0))
    got(TVR, tv_half(x2, 0))
    got(TVR + 1, tv_half(x2, 1))
    for k, step in enumerate((0, -1, 1, -2, 2, -3, 3, 4)):
        got(SD + k, chunk(step, 1 - c))
    listing.wait()

    def products(group, carry):
        for s in range(16):
            src = metas[group, 0, s]
            cls = metas[group, 1, s]
            rhs[s * 128 : (s + 1) * 128, 0:128] = sb[0, src]
            rhs[s * 128 : (s + 1) * 128, 128:256] = sb[1, src]
            values = tvb[group, s].astype(F32)
            for k in range(6):
                on = jnp.where(cls == k, 1.0, 0.0).astype(F32)
                lhs[k * 128 : (k + 1) * 128, s * 128 : (s + 1) * 128] = (values * on).astype(BF)
        prod = jnp.dot(lhs[...], rhs[...], preferred_element_type=F32).astype(BF)
        for k in range(6):
            dst, r = divmod(k, 3)
            first = pl.multiple_of((group * 3 + r) * 256, 256)
            ab[dst * 128 : (dst + 1) * 128, pl.ds(first, 256)] = prod[k * 128 : (k + 1) * 128]
        return carry

    lax.fori_loop(0, 4, products, 0)

    for d in (1, 3, 2):
        weights_end(d)
    for d in range(4):
        for k, v in enumerate((y, ym, yp, y2)):
            got(WD + 4 * k + d, whole_block(d, v, 1 - c))

    own = None
    for dx in (2, 1, 3, 0):
        quarter = turn(x, dx, 4)
        cols = pl.ds(pl.multiple_of(quarter * 256, 256), 256)
        part = jnp.dot(
            ab[...], wb[:, :, :, :, cols].reshape(3072, 256), preferred_element_type=F32
        )
        pb[dx, 0] = part[:, 0:128].astype(BF)
        pb[dx, 1] = part[:, 128:256].astype(BF)
        for other in (1, 0):
            if dx == 0 and other == 0:
                continue
            zz = zh * 2 + (zl if other == 0 else 1 - zl)
            to = lax.rem(zz, 2)
            send(PT + dx * 2 + other, pb.at[dx, to], qb.at[dx, other], at(x_=quarter, z_=zz))
    got(GR, rb.at[x2, 0])
    got(GR + 1, rb.at[x2, 1])
    rb[x, 0] = sb[0, pl.ds(own_t, 2)]
    rb[x, 1] = sb[1, pl.ds(own_t, 2)]
    gate = jnp.zeros((256, 128), F32)
    for q in range(4):
        rows = jnp.concatenate([rb[q, 0].reshape(256, 128), rb[q, 1].reshape(256, 128)], axis=1)
        gate = gate + jnp.dot(rows, gw_ref[q * 256 : (q + 1) * 256, :], preferred_element_type=F32)
    gate_open = jax.nn.sigmoid(gate + gb_ref[...])
    hidden = sb[zl, pl.ds(own_t, 2)].reshape(256, 128).astype(F32)
    message = pb[0, zl].astype(F32)
    for dx in (0, 1, 3, 2):
        for other in (0, 1):
            if dx == 0 and other == 0:
                continue
            got(PT + dx * 2 + other, qb.at[dx, other])
            message = message + qb[dx, other].astype(F32)
    update = jnp.tanh(message + ub_ref[...])
    out_ref[...] = ((1.0 - gate_open) * hidden + gate_open * update).astype(BF)

    for d in pending:
        d.wait_send()
    for k in range(9):
        copy(WX + k, wz.at[0, 0], wb.at[0, 0, 0], dxp).wait_send()


def shards(state, rel_weight, gate_weight, gate_bias, update_bias, tile_values, tile_index, tile_count):
    src, dst, r = tile_index[0, 0], tile_index[0, 1], tile_index[0, 2]
    place = src // 16 * 16 + (src // 2) % 2 * 8 + (src // 4) % 4 * 2 + src % 2
    live = jnp.arange(16, dtype=jnp.int32) < tile_count[0, 0]
    target = jnp.where(live, dst * 3 + r, 6)
    meta = jnp.pad(jnp.stack([place, target]), ((0, 6), (0, 112)))
    vmem = pl.BlockSpec(memory_space=pltpu.VMEM)
    hbm = pl.BlockSpec(memory_space=pl.ANY)
    return pl.pallas_call(
        kernel,
        out_shape=jax.ShapeDtypeStruct((256, 128), BF),
        in_specs=[hbm] * 4 + [vmem] * 3,
        out_specs=vmem,
        scratch_shapes=[
            pltpu.VMEM((4, 16, 128, 128), BF),
            pltpu.VMEM((4, 8, 128), jnp.int32),
            pltpu.SMEM((4, 8, 128), jnp.int32),
            pltpu.VMEM((2, 64, 128, 128), BF),
            pltpu.VMEM((4, 2, 2, 128, 128), BF),
            pltpu.VMEM((4, 3, 32, 1024), BF),
            pltpu.VMEM((4, 3, 8, 32, 1024), BF),
            pltpu.VMEM((768, 2048), BF),
            pltpu.VMEM((2048, 256), BF),
            pltpu.VMEM((256, 3072), BF),
            pltpu.VMEM((4, 2, 256, 128), BF),
            pltpu.VMEM((4, 2, 256, 128), BF),
            pltpu.SemaphoreType.DMA((S.total,)),
            pltpu.SemaphoreType.DMA((S.total,)),
            pltpu.SemaphoreType.DMA((5,)),
        ],
        compiler_params=pltpu.CompilerParams(
            collective_id=0, has_side_effects=True, vmem_limit_bytes=48 * 1024 * 1024
        ),
    )(
        meta, state.reshape(2, 128, 128), rel_weight, tile_values[0], gate_weight,
        gate_bias.reshape(1, 128), update_bias.reshape(1, 128),
    )


def solution(mesh):
    from jax.sharding import PartitionSpec as P

    in_specs = (
        P("ent", "rel"),
        P("rel", "ent", None),
        P(None, "rel"),
        P("rel"),
        P("rel"),
        P("rel", "ent", None, None),
        P("rel", None, "ent"),
        P("rel", "ent"),
    )
    return jax.shard_map(
        shards, mesh=mesh, in_specs=in_specs, out_specs=P("ent", "rel"), check_vma=False
    )
```

time: 250 us -> 76.3 us (0.31)
  waiting for transfers between devices: 137 us -> 0 us
  Pallas kernels: 0 us -> 69.6 us
  local copies, waits for them, and re-layouts: 45 us -> 5.71 us
  blocking collectives: 28.4 us -> 0 us
  matrix products: 23.6 us -> 0 us
  between operations: 14.1 us -> 0.7 us
    all_gather x2 -> x0, waiting for transfers between devices: 136 us -> none  [the longest x1 128 us: shards(): gathered = lax.all_gather(own_rows, 'ent', axis=0, tiled=True)]
    pallas_call x0 -> x1, Pallas kernels: none -> 69.6 us  [shards(): pl.pallas_call(kernel, out_shape=jax.ShapeDtypeStruct((256, 128), BF), in...]
    all_to_all x2 -> x0, blocking collectives: 28.4 us -> none  [the longest x1 15.3 us: copy_for_each(): lax.all_to_all(jnp.broadcast_to(x[None], (count, *x.shape)), axis, 0, 0,...]
    dot_general x6 -> x0, matrix products: 23.6 us -> none  [the longest x2 16.6 us: accumulate(): jnp.einsum('sk,sih->kih', select, product, precision=lax.Precision.HIGHEST)]
    unnamed x14 -> x15, local copies, waits for them, and re-layouts: 23 us -> 5.71 us
    gather x2 -> x0, local copies, waits for them, and re-layouts: 13.1 us -> none  [accumulate(): sources = stacked[picked[0]]]
    while x1 -> x0, local copies, waits for them, and re-layouts: 3.92 us -> none  [collect(): return lax.fori_loop(0, turn_total, accumulate, initial)]
    broadcast_in_dim x2 -> x0, local copies, waits for them, and re-layouts: 3.42 us -> none  [the longest x1 2.47 us: collect(): initial = jnp.zeros((classes, tile_rows, features), jnp.float32)]
  transfers between devices with their start and end apart: 2 -> 0, of which waited for: 2 -> 0; matrix products, arithmetic and copies ran while one was open for 25% -> 0% of each run, Pallas kernels for 0% -> 0%
where the time goes in v1:
time: 76.3 us; the launch traced here: 76 us
  Pallas kernels  69.6 us (91%)
  local copies, waits for them, and re-layouts  5.71 us (7%)
    pallas_call x1, Pallas kernels, shards(): pl.pallas_call(kernel, out_shape=jax.ShapeDtypeStruct((256, 128), BF), in...  69.6 us
    unnamed x15, local copies, waits for them, and re-layouts  5.71 us

profile of v1, /device:TPU:1, one launch (start us, length us, event | category | flops | bytes accessed | tf_op | source)
XLA Modules:
  0.0 76.0 jit_solution(3026904068259565532)
XLA Ops:
  0.7 0.0 copy-start.6
  0.7 0.7 copy-done.6
  1.4 0.0 copy-start.4
  1.4 0.0 copy-start.5
  1.4 0.6 copy-done.4
  2.0 0.0 copy-done.5
  2.0 0.0 copy-start
  2.0 1.0 %copy-done = bf16[1,16,128,128]{3,2,1,0:T(8,128)(2,1)S(1)} copy-done((bf16[1,16,128,128]{3,2,1,0:T(8,128)(2,1)S(1)}, bf16[1,16,128,128]{3,2,1,0:T(8,128)(2,1)}, u32[]{:S(2)}) %copy-start) | copy-done | bytes 524312
  3.1 0.0 copy-start.1
  3.1 0.9 %copy-done.1 = bf16[1024,128]{1,0:T(8,128)(2,1)S(1)} copy-done((bf16[1024,128]{1,0:T(8,128)(2,1)S(1)}, bf16[1024,128]{1,0:T(8,128)(2,1)}, u32[]{:S(2)}) %copy-start.1) | copy-done | bytes 262168
  4.0 0.0 copy-start.2
  4.0 0.9 %copy-done.2 = bf16[3,32,1024]{2,1,0:T(8,128)(2,1)S(1)} copy-done((bf16[3,32,1024]{2,1,0:T(8,128)(2,1)S(1)}, bf16[3,32,1024]{2,1,0:T(8,128)(2,1)}, u32[]{:S(2)}) %copy-start.2) | copy-done | bytes 196632
  5.0 0.0 copy-start.3
  5.0 0.8 %copy-done.3 = bf16[256,128]{1,0:T(8,128)(2,1)S(1)} copy-done((bf16[256,128]{1,0:T(8,128)(2,1)S(1)}, bf16[256,128]{1,0:T(8,128)(2,1)}, u32[]{:S(2)}) %copy-start.3) | copy-done | bytes 65560
  5.8 69.6 %shard_map.82 = bf16[256,128]{1,0:T(8,128)(2,1)S(1)} custom-call(s32[8,128]{1,0:T(8,128)S(1)} %pad.4.meta_in, bf16[2,128,128]{2,1,0:T(8,128)(2,1)S(1)} %bitcast.27, bf16[3,32,1024]{2,1,0:T(8,128)(2,1)S(1)} %copy-done.2, bf16[16,128,128]{2,1,0:T(8,128)(2,1)S(1)} %bitcast.26, bf16[1024,128]{1,0:T(8,128)(2,1)S(1)} %copy-done.1, f32[1,128]{1,0:T(1,128)S(1)} %bitcast.28, ...), custom_call_target="tpu_custom_call" | custom-call | tf_op jit(solution)/shard_map/pallas_call | solution.py:331
  75.4 0.6 copy.11
  (3 shorter events, 0.0 us)
Async XLA Ops:
  0.7 0.7 copy-start.6
  1.4 0.7 copy-start.4
  1.4 0.7 copy-start.5
  2.0 1.0 %copy-start = (bf16[1,16,128,128]{3,2,1,0:T(8,128)(2,1)S(1)}, bf16[1,16,128,128]{3,2,1,0:T(8,128)(2,1)}, u32[]{:S(2)}) copy-start(bf16[1,16,128,128]{3,2,1,0:T(8,128)(2,1)} %param.13) | copy-start | bytes 1572868
  3.1 0.9 %copy-start.1 = (bf16[1024,128]{1,0:T(8,128)(2,1)S(1)}, bf16[1024,128]{1,0:T(8,128)(2,1)}, u32[]{:S(2)}) copy-start(bf16[1024,128]{1,0:T(8,128)(2,1)} %gw_ref.1) | copy-start | bytes 786436
  4.0 0.9 %copy-start.2 = (bf16[3,32,1024]{2,1,0:T(8,128)(2,1)S(1)}, bf16[3,32,1024]{2,1,0:T(8,128)(2,1)}, u32[]{:S(2)}) copy-start(bf16[3,32,1024]{2,1,0:T(8,128)(2,1)} %relw_in.1) | copy-start | bytes 589828
  5.0 0.8 %copy-start.3 = (bf16[256,128]{1,0:T(8,128)(2,1)S(1)}, bf16[256,128]{1,0:T(8,128)(2,1)}, u32[]{:S(2)}) copy-start(bf16[256,128]{1,0:T(8,128)(2,1)} %param.8) | copy-start | bytes 196612

commit v2 on v1

v2 whole, which is shorter than its diff:
```python
import jax
import jax.numpy as jnp
from jax import lax
from jax.experimental import pallas as pl
from jax.experimental.pallas import tpu as pltpu

MESH = pl.DeviceIdType.MESH
BF = jnp.bfloat16
F32 = jnp.float32


class Sems:
    def __init__(self):
        self.total = 0

    def take(self, count):
        first = self.total
        self.total += count
        return first


S = Sems()
TVP, TVM, TVR = S.take(2), S.take(2), S.take(2)
MET = S.take(3)
SY, SYR = S.take(2), S.take(2)
SZP, SZM = S.take(16), S.take(16)
SD = S.take(8)
GP, GM, GR = S.take(2), S.take(2), S.take(2)
WZP, WZM, WZR0, WZR1 = S.take(4), S.take(4), S.take(4), S.take(4)
WX = S.take(16)
DS = S.take(8)
WYP, WYM, WYR0, WYR1 = S.take(16), S.take(16), S.take(16), S.take(16)
WD = S.take(28)
PT = S.take(8)

QUARTERS = (2, 1, 3, 0)


def kernel(
    meta_in, state_in, relw_in, tv_in, gw_in, gb_in, ub_in, out_ref,
    gw_ref, gb_ref, ub_ref, gate_ref, tvb, metav, metas, sb, rb, wz, wb, cb, ab, pb, qb, ssem, rsem, lsem,
):
    rel = lax.axis_index("rel")
    ent = lax.axis_index("ent")
    x, zl = lax.div(rel, 2), lax.rem(rel, 2)
    zh, y, c = lax.div(ent, 8), lax.rem(lax.div(ent, 2), 4), lax.rem(ent, 2)
    z = zh * 2 + zl

    def turn(v, step, count):
        return lax.rem(v + (step + count) % count, count)

    def at(x_=None, y_=None, z_=None, c_=None):
        xx = x if x_ is None else x_
        yy = y if y_ is None else y_
        zz = z if z_ is None else z_
        cc = c if c_ is None else c_
        return (xx * 2 + lax.rem(zz, 2), lax.div(zz, 2) * 8 + yy * 2 + cc)

    xp, xm, x2 = turn(x, 1, 4), turn(x, -1, 4), turn(x, 2, 4)
    yp, ym, y2 = turn(y, 1, 4), turn(y, -1, 4), turn(y, 2, 4)
    hp, hm, h2 = turn(zh, 1, 4), turn(zh, -1, 4), turn(zh, 2, 4)
    zo = zh * 2 + (1 - zl)
    dxp, dxm, dx2 = at(x_=xp), at(x_=xm), at(x_=x2)
    dyp, dym = at(y_=yp), at(y_=ym)
    dzp, dzm = at(z_=turn(z, 1, 8)), at(z_=turn(z, -1, 8))
    dhp, dhm = at(z_=hp * 2 + zl), at(z_=hm * 2 + zl)
    dco = at(c_=1 - c)
    peers = [dxp, dxm, dx2, dyp, dym, dzp, dzm, dhp, dhm, dco]
    peers += [at(x_=v, z_=zo) for v in (xp, xm, x2)]
    away = zh != x
    targets = [at(x_=zh, z_=v * 2 + zl) for v in (h2, hp, hm, zh)]
    sources = [at(x_=v, z_=x * 2 + zl) for v in (x2, xp, xm, x)]

    pending = []

    def copy(i, src, dst, dev, there=None):
        return pltpu.make_async_remote_copy(
            src_ref=src, dst_ref=dst, send_sem=ssem.at[i],
            recv_sem=rsem.at[i if there is None else there],
            device_id=dev, device_id_type=MESH,
        )

    def send(i, src, dst, dev):
        d = copy(i, src, dst, dev)
        d.start()
        pending.append(d)

    def got(i, ref):
        copy(i, ref, ref, dco).wait_recv()

    yc = y * 2 + c
    own_t = ((zh * 2 + c) * 4 + y) * 2

    local = [
        pltpu.make_async_copy(state_in, sb.at[zl, pl.ds(own_t, 2)], lsem.at[1]),
        pltpu.make_async_copy(meta_in, metav.at[x], lsem.at[2]),
        pltpu.make_async_copy(tv_in, tvb.at[x], lsem.at[3]),
    ]
    for k in range(4):
        for j in range(2):
            cols = (turn(zh, QUARTERS[k], 4) * 2 + j) * 128
            local.append(
                pltpu.make_async_copy(
                    relw_in.at[:, :, pl.ds(pl.multiple_of(cols, 128), 128)],
                    wz.at[zh, k, j], lsem.at[8 + k * 2 + j],
                )
            )
    late = [
        pltpu.make_async_copy(gw_in, gw_ref, lsem.at[5]),
        pltpu.make_async_copy(gb_in, gb_ref, lsem.at[6]),
        pltpu.make_async_copy(ub_in, ub_ref, lsem.at[7]),
    ]
    for d in local + late:
        d.start()
    barrier = pltpu.get_barrier_semaphore()
    for dev in peers:
        pl.semaphore_signal(barrier, inc=1, device_id=dev, device_id_type=MESH)
    for dev in targets[:3] + sources[:3]:
        pl.semaphore_signal(barrier, inc=1, device_id=dev, device_id_type=MESH)

    @pl.when(away)
    def _():
        for dev in (targets[3], sources[3]):
            pl.semaphore_signal(barrier, inc=1, device_id=dev, device_id_type=MESH)

    for d in local:
        d.wait()
    pl.semaphore_wait(barrier, len(peers) + 6 + 2 * jnp.where(away, 1, 0))

    def weights_first(k):
        send(WZP + k, wz.at[zh, k], wz.at[zh, k], dhp)
        send(WZM + k, wz.at[zh, k], wz.at[zh, k], dhm)

    def weight_row(slot, k):
        d = lax.rem(slot - x + 4, 4)

        @pl.when(d != 0)
        def _():
            copy(
                WX + d * 4 + k, wz.at[slot, k], wb.at[k, :, x, :, yc], at(x_=slot)
            ).start()

    def weights_direct(k):
        to = WX + lax.rem(zh - x + 4, 4) * 4 + k
        for i in range(3):
            d = copy(DS + k * 4 + i, wz.at[zh, k], wb.at[k, :, x, :, yc], targets[i], to)
            d.start()
            pending.append(d)

        @pl.when(away)
        def _():
            copy(DS + k * 4 + 3, wz.at[zh, k], wb.at[k, :, x, :, yc], targets[3], to).start()

    def tv_half(x_, h):
        return tvb.at[x_, pl.ds(h * 8, 8)]

    order_y = (y, ym, yp, y2)

    def piece(step, j, cc=None, first=0, count=2):
        zz = turn(z, step, 8)
        place = (lax.div(zz, 2) * 2 + (c if cc is None else cc)) * 4 + order_y[j]
        return sb.at[lax.rem(zz, 2), pl.ds(place * 2 + first, count)]

    def chunk(step, cc):
        zz = turn(z, step, 8)
        return sb.at[lax.rem(zz, 2), pl.ds((lax.div(zz, 2) * 2 + cc) * 8, 8)]

    def share(k, step):
        send(SD + k, chunk(step, c), chunk(step, c), dco)

    def state_first(j):
        send(SZP + j, piece(0, j), piece(0, j), dzp)
        send(SZM + j, piece(0, j), piece(0, j), dzm)

    def state_on(k, j):
        got(SZP + (k - 1) * 4 + j, piece(-k, j))
        got(SZM + (k - 1) * 4 + j, piece(k, j))
        first, count = (0, 2) if k < 3 else (0, 1)
        ref = piece(-k, j, None, first, count)
        send(SZP + k * 4 + j, ref, ref, dzp)
        ref = piece(k, j, None, first if k < 3 else 1, count)
        send(SZM + k * 4 + j, ref, ref, dzm)

    def weights_far(k):
        got(WZP + k, wz.at[hm, k])
        send(WZR0 + k, wz.at[hm, k, 0], wz.at[hm, k, 0], dhp)
        got(WZM + k, wz.at[hp, k])
        send(WZR1 + k, wz.at[hp, k, 1], wz.at[hp, k, 1], dhm)
        weight_row(hm, k)
        weight_row(hp, k)

    def weights_last(k):
        got(WZR0 + k, wz.at[h2, k, 0])
        got(WZR1 + k, wz.at[h2, k, 1])
        weight_row(h2, k)

    def block(d, k, y_, cc=None):
        return wb.at[k, :, turn(x, -d, 4), :, y_ * 2 + (c if cc is None else cc)]

    def half_block(d, k, y_, h):
        return wb.at[k, h, turn(x, -d, 4), :, y_ * 2 + c]

    def all_blocks(k, y_, cc=None):
        return wb.at[k, :, :, :, y_ * 2 + (c if cc is None else cc)]

    def weights_out(d, k):
        dst = block(d, k, y)

        def spread(src):
            send(WYP + d * 4 + k, src, dst, dyp)
            send(WYM + d * 4 + k, src, dst, dym)
            send(WD + d * 4 + k, src, dst, dco)

        if d == 0 and k < 2:

            @pl.when(away)
            def _():
                got(WX + k, dst)
                spread(dst)
                del pending[-3:]

            @pl.when(jnp.logical_not(away))
            def _():
                spread(wz.at[x, k])
                del pending[-3:]

            for i in (WYP, WYM, WD):
                pending.append(copy(i + k, wz.at[x, k], dst, dco))
        elif d == 0:
            spread(wz.at[x, k])
        else:
            got(WX + d * 4 + k, dst)
            spread(dst)

    def weights_on(d, k):
        got(WYP + d * 4 + k, block(d, k, ym))
        send(WYR0 + d * 4 + k, half_block(d, k, ym, 0), half_block(d, k, ym, 0), dyp)
        got(WYM + d * 4 + k, block(d, k, yp))
        send(WYR1 + d * 4 + k, half_block(d, k, yp, 1), half_block(d, k, yp, 1), dym)

    def weights_end(d, k):
        got(WYR0 + d * 4 + k, half_block(d, k, y2, 0))
        got(WYR1 + d * 4 + k, half_block(d, k, y2, 1))

    groups = (0, 1, 3, 2)

    def outs(k):
        for d in groups:
            weights_out(d, k)

    def ons(k):
        for d in groups:
            weights_on(d, k)
        send(WD + 16 + k, all_blocks(k, ym), all_blocks(k, ym), dco)
        send(WD + 20 + k, all_blocks(k, yp), all_blocks(k, yp), dco)

    def ends(k):
        for d in groups:
            weights_end(d, k)
        send(WD + 24 + k, all_blocks(k, y2), all_blocks(k, y2), dco)

    def partner(k):
        for d in groups:
            got(WD + d * 4 + k, block(d, k, y, 1 - c))
        for i, v in enumerate((ym, yp, y2)):
            got(WD + 16 + 4 * i + k, all_blocks(k, v, 1 - c))

    weights_direct(0)
    mine = piece(0, 0)
    send(SY, mine, mine, dyp)
    send(SY + 1, mine, mine, dym)
    weights_direct(1)
    for k in (2, 3):
        weight_row(zh, k)
    weights_first(2)
    weights_first(3)
    state_first(0)
    for k, dev in enumerate((dxp, dxm, dx2)):
        send(MET + k, metav.at[x], metav.at[x], dev)
    send(TVP, tv_half(x, 0), tv_half(x, 0), dxp)
    send(TVM + 1, tv_half(x, 1), tv_half(x, 1), dxm)

    got(SY, piece(0, 1))
    send(SYR, piece(0, 1, None, 0, 1), piece(0, 1, None, 0, 1), dyp)
    got(SY + 1, piece(0, 2))
    send(SYR + 1, piece(0, 2, None, 1, 1), piece(0, 2, None, 1, 1), dym)

    outs(0)
    weights_far(2)
    state_first(1)
    state_first(2)
    weights_far(3)
    got(SYR, piece(0, 3, None, 0, 1))
    got(SYR + 1, piece(0, 3, None, 1, 1))
    state_first(3)
    share(0, 0)
    outs(1)
    weights_last(2)
    state_on(1, 0)
    weights_last(3)
    state_on(1, 1)
    state_on(1, 2)
    ons(0)
    state_on(1, 3)
    share(1, -1)
    share(2, 1)
    send(TVP + 1, tv_half(x, 1), tv_half(x, 1), dxp)
    send(TVM, tv_half(x, 0), tv_half(x, 0), dxm)
    for q in range(2):
        pair = sb.at[q, pl.ds(own_t, 2)]
        send(GP + q, pair, rb.at[x, q], dxp)
        send(GM + q, pair, rb.at[x, q], dxm)
    state_on(2, 0)
    outs(2)
    state_on(2, 1)
    state_on(2, 2)
    ons(1)
    state_on(2, 3)
    share(3, -2)
    share(4, 2)
    got(TVP, tv_half(xm, 0))
    send(TVR, tv_half(xm, 0), tv_half(xm, 0), dxp)
    got(TVM + 1, tv_half(xp, 1))
    send(TVR + 1, tv_half(xp, 1), tv_half(xp, 1), dxm)
    outs(3)
    state_on(3, 0)
    state_on(3, 1)
    for k in (2, 3):
        wb[k, :, x, :, yc] = wz[x, k]

    @pl.when(jnp.logical_not(away))
    def _():
        for k in (0, 1):
            wb[k, :, x, :, yc] = wz[x, k]

    cb[16] = jnp.zeros((128, 256), F32)
    for q in range(2):
        got(GP + q, rb.at[xm, q])
        got(GM + q, rb.at[xp, q])
    send(GR, rb.at[xm, 0], rb.at[xm, 0], dxp)
    send(GR + 1, rb.at[xp, 1], rb.at[xp, 1], dxm)
    ons(2)
    state_on(3, 2)
    state_on(3, 3)
    share(5, -3)
    share(6, 3)
    ends(0)
    for k, v in enumerate((xm, xp, x2)):
        got(MET + k, metav.at[v])
    listing = pltpu.make_async_copy(metav, metas, lsem.at[4])
    listing.start()
    ons(3)
    ends(1)
    got(GR, rb.at[x2, 0])
    got(GR + 1, rb.at[x2, 1])
    rb[x, 0] = sb[0, pl.ds(own_t, 2)]
    rb[x, 1] = sb[1, pl.ds(own_t, 2)]
    for d in late:
        d.wait()
    gate = jnp.zeros((256, 128), F32)
    for q in range(4):
        rows = jnp.concatenate([rb[q, 0].reshape(256, 128), rb[q, 1].reshape(256, 128)], axis=1)
        gate = gate + jnp.dot(rows, gw_ref[q * 256 : (q + 1) * 256, :], preferred_element_type=F32)
    gate_ref[...] = jax.nn.sigmoid(gate + gb_ref[...])
    for j in range(4):
        got(SZP + 12 + j, piece(4, j, None, 0, 1))
        got(SZM + 12 + j, piece(4, j, None, 1, 1))
    share(7, 4)
    got(TVP + 1, tv_half(xm, 1))
    got(TVM, tv_half(xp, 0))
    got(TVR, tv_half(x2, 0))
    got(TVR + 1, tv_half(x2, 1))
    for k, step in enumerate((0, -1, 1, -2, 2, -3, 3, 4)):
        got(SD + k, chunk(step, 1 - c))
    listing.wait()

    def products(group, carry):
        last = [jnp.int32(16)] * 6
        for t in range(16):
            src = metas[group, 0, t]
            cls = metas[group, 1, t]
            prev = jnp.int32(16)
            for k in range(6):
                prev = jnp.where(cls == k, last[k], prev)
                last[k] = jnp.where(cls == k, t, last[k])
            rows = jnp.concatenate([sb[0, src], sb[1, src]], axis=1)
            cb[t] = jnp.dot(tvb[group, t], rows, preferred_element_type=F32) + cb[prev]
        for k in range(6):
            dst, r = divmod(k, 3)
            first = pl.multiple_of((group * 3 + r) * 256, 256)
            ab[dst * 128 : (dst + 1) * 128, pl.ds(first, 256)] = cb[last[k]].astype(BF)
        return carry

    lax.fori_loop(0, 4, products, 0)

    for k, dx in enumerate(QUARTERS):
        if k >= 2:
            ends(k)
        partner(k)
        quarter = turn(x, dx, 4)
        cols = jnp.concatenate([wb[k, 0].reshape(3072, 128), wb[k, 1].reshape(3072, 128)], axis=1)
        part = jnp.dot(ab[...], cols, preferred_element_type=F32)
        pb[dx, 0] = part[:, 0:128].astype(BF)
        pb[dx, 1] = part[:, 128:256].astype(BF)
        for other in (1, 0):
            if dx == 0 and other == 0:
                continue
            zz = zh * 2 + (zl if other == 0 else 1 - zl)
            to = lax.rem(zz, 2)
            send(PT + dx * 2 + other, pb.at[dx, to], qb.at[dx, other], at(x_=quarter, z_=zz))
    hidden = sb[zl, pl.ds(own_t, 2)].reshape(256, 128).astype(F32)
    message = pb[0, zl].astype(F32)
    for dx in QUARTERS:
        for other in (0, 1):
            if dx == 0 and other == 0:
                continue
            got(PT + dx * 2 + other, qb.at[dx, other])
            message = message + qb[dx, other].astype(F32)
    update = jnp.tanh(message + ub_ref[...])
    gate_open = gate_ref[...]
    out_ref[...] = ((1.0 - gate_open) * hidden + gate_open * update).astype(BF)

    for d in pending:
        d.wait_send()
    for d in range(1, 4):
        for k in (2, 3):
            copy(WX + d * 4 + k, wz.at[0, 0], wb.at[0, :, 0, :, 0], dxp).wait_send()

    @pl.when(away)
    def _():
        for k in (0, 1):
            copy(DS + k * 4 + 3, wz.at[0, 0], wb.at[0, :, 0, :, 0], dxp).wait_send()


def shards(state, rel_weight, gate_weight, gate_bias, update_bias, tile_values, tile_index, tile_count):
    src, dst, r = tile_index[0, 0], tile_index[0, 1], tile_index[0, 2]
    place = src // 16 * 16 + (src // 2) % 2 * 8 + (src // 4) % 4 * 2 + src % 2
    live = jnp.arange(16, dtype=jnp.int32) < tile_count[0, 0]
    target = jnp.where(live, dst * 3 + r, 6)
    meta = jnp.pad(jnp.stack([place, target]), ((0, 6), (0, 112)))
    vmem = pl.BlockSpec(memory_space=pltpu.VMEM)
    hbm = pl.BlockSpec(memory_space=pl.ANY)
    return pl.pallas_call(
        kernel,
        out_shape=jax.ShapeDtypeStruct((256, 128), BF),
        in_specs=[hbm] * 7,
        out_specs=vmem,
        scratch_shapes=[
            pltpu.VMEM((1024, 128), BF),
            pltpu.VMEM((1, 128), F32),
            pltpu.VMEM((1, 128), F32),
            pltpu.VMEM((256, 128), F32),
            pltpu.VMEM((4, 16, 128, 128), BF),
            pltpu.VMEM((4, 8, 128), jnp.int32),
            pltpu.SMEM((4, 8, 128), jnp.int32),
            pltpu.VMEM((2, 64, 128, 128), BF),
            pltpu.VMEM((4, 2, 2, 128, 128), BF),
            pltpu.VMEM((4, 4, 2, 3, 32, 128), BF),
            pltpu.VMEM((4, 2, 4, 3, 8, 32, 128), BF),
            pltpu.VMEM((17, 128, 256), F32),
            pltpu.VMEM((256, 3072), BF),
            pltpu.VMEM((4, 2, 256, 128), BF),
            pltpu.VMEM((4, 2, 256, 128), BF),
            pltpu.SemaphoreType.DMA((S.total,)),
            pltpu.SemaphoreType.DMA((S.total,)),
            pltpu.SemaphoreType.DMA((16,)),
        ],
        compiler_params=pltpu.CompilerParams(
            collective_id=0, has_side_effects=True, vmem_limit_bytes=62 * 1024 * 1024
        ),
    )(
        meta, state.reshape(2, 128, 128), rel_weight, tile_values[0], gate_weight,
        gate_bias.reshape(1, 128), update_bias.reshape(1, 128),
    )


def solution(mesh):
    from jax.sharding import PartitionSpec as P

    in_specs = (
        P("ent", "rel"),
        P("rel", "ent", None),
        P(None, "rel"),
        P("rel"),
        P("rel"),
        P("rel", "ent", None, None),
        P("rel", None, "ent"),
        P("rel", "ent"),
    )
    return jax.shard_map(
        shards, mesh=mesh, in_specs=in_specs, out_specs=P("ent", "rel"), check_vma=False
    )
```

time: 76.3 us -> 71 us (0.931)
  local copies, waits for them, and re-layouts: 5.71 us -> 2.75 us
  Pallas kernels: 69.6 us -> 67.4 us
    unnamed x15 -> x3, local copies, waits for them, and re-layouts: 5.71 us -> 2.15 us
    pallas_call x1, Pallas kernels: 69.6 us -> 67.4 us  [shards(): pl.pallas_call(kernel, out_shape=jax.ShapeDtypeStruct((256, 128), BF), in...]
where the time goes in v2:
time: 71 us; the launch traced here: 70.8 us
  Pallas kernels  67.4 us (95%)
  local copies, waits for them, and re-layouts  2.75 us (4%)
    pallas_call x1, Pallas kernels, shards(): pl.pallas_call(kernel, out_shape=jax.ShapeDtypeStruct((256, 128), BF), in...  67.4 us
    unnamed x3, local copies, waits for them, and re-layouts  2.15 us

profile of v2, /device:TPU:1, one launch (start us, length us, event | category | flops | bytes accessed | tf_op | source)
XLA Modules:
  0.0 70.8 jit_solution(9373682672544994370)
XLA Ops:
  0.7 0.0 copy-start
  0.7 0.7 copy-done
  1.4 0.6 pad.4.meta_in
  2.0 67.4 %shard_map.82 = bf16[256,128]{1,0:T(8,128)(2,1)} custom-call(s32[8,128]{1,0:T(8,128)} %pad.4.meta_in, bf16[2,128,128]{2,1,0:T(8,128)(2,1)} %bitcast.27, bf16[3,32,1024]{2,1,0:T(8,128)(2,1)} %relw_in.1, bf16[16,128,128]{2,1,0:T(8,128)(2,1)} %bitcast.26, bf16[1024,128]{1,0:T(8,128)(2,1)} %gw_in.1, f32[1,128]{1,0:T(1,128)} %bitcast.28, f32[1,128]{1,0:T(1,128)} %bitcast.29), custom_call_target="tpu_custom_call" | custom-call | tf_op jit(solution)/shard_map/pallas_call | solution.py:443
  69.4 1.5 %copy.11 = bf16[256,128]{1,0:T(8,128)(2,1)} copy(bf16[256,128]{1,0:T(8,128)(2,1)} %shard_map.82) | data formatting | bytes 131072
  (2 shorter events, 0.0 us)
Async XLA Ops:
  0.7 0.7 copy-start

commit v3 on v2

v3 whole, which is shorter than its diff:
```python
import jax
import jax.numpy as jnp
from jax import lax
from jax.experimental import pallas as pl
from jax.experimental.pallas import tpu as pltpu

MESH = pl.DeviceIdType.MESH
BF = jnp.bfloat16
F32 = jnp.float32


class Sems:
    def __init__(self):
        self.total = 0

    def take(self, count):
        first = self.total
        self.total += count
        return first


S = Sems()
TVP, TVM, TVR = S.take(4), S.take(4), S.take(4)
MET = S.take(3)
SY, SYR = S.take(2), S.take(2)
SZP, SZM = S.take(16), S.take(16)
SD, SE = S.take(8), S.take(8)
VZP, VZM = S.take(4), S.take(4)
VYP, VYM, VYR0, VYR1 = S.take(8), S.take(8), S.take(8), S.take(8)
GP, GM, GR = S.take(2), S.take(2), S.take(2)
WZP, WZM, WZR0, WZR1 = S.take(4), S.take(4), S.take(4), S.take(4)
WX = S.take(12)
WYP, WYM, WYR0, WYR1 = S.take(16), S.take(16), S.take(16), S.take(16)
WD = S.take(28)
PT = S.take(8)

QUARTERS = (2, 1, 3, 0)


def kernel(
    meta_in, state_in, relw_in, tv_in, gw_in, gb_in, ub_in, out_ref,
    gw_ref, gb_ref, ub_ref, gate_ref, tvb, metav, metas, sb, rb, wz, wb, cb, ab, pb, qb, ssem, rsem, lsem,
):
    rel = lax.axis_index("rel")
    ent = lax.axis_index("ent")
    x, zl = lax.div(rel, 2), lax.rem(rel, 2)
    zh, y, c = lax.div(ent, 8), lax.rem(lax.div(ent, 2), 4), lax.rem(ent, 2)
    z = zh * 2 + zl

    def turn(v, step, count):
        return lax.rem(v + (step + count) % count, count)

    def at(x_=None, y_=None, z_=None, c_=None):
        xx = x if x_ is None else x_
        yy = y if y_ is None else y_
        zz = z if z_ is None else z_
        cc = c if c_ is None else c_
        return (xx * 2 + lax.rem(zz, 2), lax.div(zz, 2) * 8 + yy * 2 + cc)

    xp, xm, x2 = turn(x, 1, 4), turn(x, -1, 4), turn(x, 2, 4)
    yp, ym, y2 = turn(y, 1, 4), turn(y, -1, 4), turn(y, 2, 4)
    hp, hm, h2 = turn(zh, 1, 4), turn(zh, -1, 4), turn(zh, 2, 4)
    zo = zh * 2 + (1 - zl)
    dxp, dxm, dx2 = at(x_=xp), at(x_=xm), at(x_=x2)
    dyp, dym = at(y_=yp), at(y_=ym)
    dzp, dzm = at(z_=turn(z, 1, 8)), at(z_=turn(z, -1, 8))
    dhp, dhm = at(z_=hp * 2 + zl), at(z_=hm * 2 + zl)
    dco = at(c_=1 - c)
    peers = [dxp, dxm, dx2, dyp, dym, dzp, dzm, dhp, dhm, dco]
    peers += [at(x_=v, z_=zo) for v in (xp, xm, x2)]

    pending = []

    def copy(i, src, dst, dev):
        return pltpu.make_async_remote_copy(
            src_ref=src, dst_ref=dst, send_sem=ssem.at[i], recv_sem=rsem.at[i],
            device_id=dev, device_id_type=MESH,
        )

    def send(i, src, dst, dev):
        d = copy(i, src, dst, dev)
        d.start()
        pending.append(d)

    def got(i, ref):
        copy(i, ref, ref, dco).wait_recv()

    yc = y * 2 + c
    own = zh * 2 + c

    local = [
        pltpu.make_async_copy(state_in, sb.at[zl, own, y], lsem.at[1]),
        pltpu.make_async_copy(meta_in, metav.at[x], lsem.at[2]),
        pltpu.make_async_copy(tv_in, tvb.at[x], lsem.at[3]),
    ]
    for k in range(4):
        for j in range(2):
            cols = (turn(zh, QUARTERS[k], 4) * 2 + j) * 128
            local.append(
                pltpu.make_async_copy(
                    relw_in.at[:, :, pl.ds(pl.multiple_of(cols, 128), 128)],
                    wz.at[zh, k, j], lsem.at[8 + k * 2 + j],
                )
            )
    late = [
        pltpu.make_async_copy(gw_in, gw_ref, lsem.at[5]),
        pltpu.make_async_copy(gb_in, gb_ref, lsem.at[6]),
        pltpu.make_async_copy(ub_in, ub_ref, lsem.at[7]),
    ]
    for d in local + late:
        d.start()
    barrier = pltpu.get_barrier_semaphore()
    for dev in peers:
        pl.semaphore_signal(barrier, inc=1, device_id=dev, device_id_type=MESH)
    for d in local:
        d.wait()
    pl.semaphore_wait(barrier, len(peers))

    def weights_first(k):
        send(WZP + k, wz.at[zh, k], wz.at[zh, k], dhp)
        send(WZM + k, wz.at[zh, k], wz.at[zh, k], dhm)

    def weight_row(slot, k):
        d = lax.rem(slot - x + 4, 4)

        @pl.when(d != 0)
        def _():
            copy(
                WX + (d - 1) * 4 + k, wz.at[slot, k], wb.at[k, :, x, :, yc], at(x_=slot)
            ).start()

    def tv_part(x_, h):
        return tvb.at[x_, pl.ds(h * 4, 4)]

    order_y = (y, ym, yp, y2)

    def tile(step, j, i):
        zz = turn(z, step, 8)
        rows = 3 if i == 1 else pl.ds(0, 3)
        return sb.at[lax.rem(zz, 2), lax.div(zz, 2) * 2 + c, order_y[j], rows]

    def half_tile(step, j, i, h):
        zz = turn(z, step, 8)
        place = (lax.rem(zz, 2), lax.div(zz, 2) * 2 + c, order_y[j])
        if i == 1:
            return sb.at[*place, 3, pl.ds(h * 32, 32)]
        long_first = j in (0, 3)
        cut = 2 if long_first else 1
        return sb.at[*place, pl.ds(0, cut) if h == 0 else pl.ds(cut, 3 - cut)]

    def tiles(step, i, cc):
        zz = turn(z, step, 8)
        rows = 3 if i == 1 else pl.ds(0, 3)
        return sb.at[lax.rem(zz, 2), lax.div(zz, 2) * 2 + cc, :, rows]

    def share(k, step):
        send(SD + k, tiles(step, 0, c), tiles(step, 0, c), dco)

    def y_part(y_, h):
        return sb.at[zl, own, y_, pl.ds(0, 2) if h == 0 else 2]

    def state_first(j):
        send(SZP + j, tile(0, j, 0), tile(0, j, 0), dzp)
        send(SZM + j, tile(0, j, 0), tile(0, j, 0), dzm)

    def state_on(k, j):
        got(SZP + (k - 1) * 4 + j, tile(-k, j, 0))
        got(SZM + (k - 1) * 4 + j, tile(k, j, 0))
        left = tile(-k, j, 0) if k < 3 else half_tile(-k, j, 0, 0)
        right = tile(k, j, 0) if k < 3 else half_tile(k, j, 0, 1)
        send(SZP + k * 4 + j, left, left, dzp)
        send(SZM + k * 4 + j, right, right, dzm)

    steps = (0, -1, 1, -2, 2, -3, 3, 4)

    def second_y(n):
        ref = tile(steps[n], 0, 1)
        send(VYP + n, ref, ref, dyp)
        send(VYM + n, ref, ref, dym)

    def second_z(k):
        got(VZP + k - 1, tile(-k, 0, 1))
        got(VZM + k - 1, tile(k, 0, 1))
        left = tile(-k, 0, 1) if k < 3 else half_tile(-k, 0, 1, 0)
        right = tile(k, 0, 1) if k < 3 else half_tile(k, 0, 1, 1)
        send(VZP + k, left, left, dzp)
        send(VZM + k, right, right, dzm)
        second_y(2 * k - 1)
        second_y(2 * k)

    def second_on(n):
        got(VYP + n, tile(steps[n], 1, 1))
        ref = half_tile(steps[n], 1, 1, 0)
        send(VYR0 + n, ref, ref, dyp)
        got(VYM + n, tile(steps[n], 2, 1))
        ref = half_tile(steps[n], 2, 1, 1)
        send(VYR1 + n, ref, ref, dym)

    def second_end(n):
        got(VYR0 + n, half_tile(steps[n], 3, 1, 0))
        got(VYR1 + n, half_tile(steps[n], 3, 1, 1))
        send(SE + n, tiles(steps[n], 1, c), tiles(steps[n], 1, c), dco)

    def weights_far(k):
        got(WZP + k, wz.at[hm, k])
        send(WZR0 + k, wz.at[hm, k, 0], wz.at[hm, k, 0], dhp)
        got(WZM + k, wz.at[hp, k])
        send(WZR1 + k, wz.at[hp, k, 1], wz.at[hp, k, 1], dhm)
        weight_row(hm, k)
        weight_row(hp, k)

    def weights_last(k):
        got(WZR0 + k, wz.at[h2, k, 0])
        got(WZR1 + k, wz.at[h2, k, 1])
        weight_row(h2, k)

    def block(d, k, y_, cc=None):
        return wb.at[k, :, turn(x, -d, 4), :, y_ * 2 + (c if cc is None else cc)]

    def half_block(d, k, y_, h):
        return wb.at[k, h, turn(x, -d, 4), :, y_ * 2 + c]

    def all_blocks(k, y_, cc=None):
        return wb.at[k, :, :, :, y_ * 2 + (c if cc is None else cc)]

    def weights_out(d, k):
        src = block(d, k, y)
        if d == 0:
            src = wz.at[x, k]
        else:
            got(WX + (d - 1) * 4 + k, src)
        send(WYP + d * 4 + k, src, block(d, k, y), dyp)
        send(WYM + d * 4 + k, src, block(d, k, y), dym)
        send(WD + d * 4 + k, src, block(d, k, y), dco)

    def weights_on(d, k):
        got(WYP + d * 4 + k, block(d, k, ym))
        send(WYR0 + d * 4 + k, half_block(d, k, ym, 0), half_block(d, k, ym, 0), dyp)
        got(WYM + d * 4 + k, block(d, k, yp))
        send(WYR1 + d * 4 + k, half_block(d, k, yp, 1), half_block(d, k, yp, 1), dym)

    def weights_end(d, k):
        got(WYR0 + d * 4 + k, half_block(d, k, y2, 0))
        got(WYR1 + d * 4 + k, half_block(d, k, y2, 1))

    groups = (0, 1, 3, 2)

    def outs(k):
        for d in groups:
            weights_out(d, k)

    def ons(k):
        for d in groups:
            weights_on(d, k)
        send(WD + 16 + k, all_blocks(k, ym), all_blocks(k, ym), dco)
        send(WD + 20 + k, all_blocks(k, yp), all_blocks(k, yp), dco)

    def ends(k):
        for d in groups:
            weights_end(d, k)
        send(WD + 24 + k, all_blocks(k, y2), all_blocks(k, y2), dco)

    def partner(k):
        for d in groups:
            got(WD + d * 4 + k, block(d, k, y, 1 - c))
        for i, v in enumerate((ym, yp, y2)):
            got(WD + 16 + 4 * i + k, all_blocks(k, v, 1 - c))

    def tv_send(n):
        right, left = n, (n + 2) % 4
        send(TVP + right, tv_part(x, right), tv_part(x, right), dxp)
        send(TVM + left, tv_part(x, left), tv_part(x, left), dxm)

    def tv_on(n):
        got(TVP + n, tv_part(xm, n))
        send(TVR + n, tv_part(xm, n), tv_part(xm, n), dxp)
        got(TVM + 2 + n, tv_part(xp, 2 + n))
        send(TVR + 2 + n, tv_part(xp, 2 + n), tv_part(xp, 2 + n), dxm)

    def tv_end():
        for n in range(2):
            got(TVP + 2 + n, tv_part(xm, 2 + n))
            got(TVM + n, tv_part(xp, n))
        for n in range(4):
            got(TVR + n, tv_part(x2, n))

    def gate_first():
        for q in range(2):
            pair = sb.at[q, own, y]
            send(GP + q, pair, rb.at[x, q], dxp)
            send(GM + q, pair, rb.at[x, q], dxm)

    def gate_on():
        for q in range(2):
            got(GP + q, rb.at[xm, q])
            got(GM + q, rb.at[xp, q])
        send(GR, rb.at[xm, 0], rb.at[xm, 0], dxp)
        send(GR + 1, rb.at[xp, 1], rb.at[xp, 1], dxm)

    def gate_end():
        got(GR, rb.at[x2, 0])
        got(GR + 1, rb.at[x2, 1])
        rb[x, 0] = sb[0, own, y]
        rb[x, 1] = sb[1, own, y]
        for d in late:
            d.wait()
        gate = jnp.zeros((256, 128), F32)
        for q in range(4):
            rows = jnp.concatenate(
                [rb[q, 0].reshape(256, 128), rb[q, 1].reshape(256, 128)], axis=1
            )
            gate = gate + jnp.dot(
                rows, gw_ref[q * 256 : (q + 1) * 256, :], preferred_element_type=F32
            )
        gate_ref[...] = jax.nn.sigmoid(gate + gb_ref[...])

    listing = pltpu.make_async_copy(metav, metas, lsem.at[4])

    def products(group, carry):
        last = [jnp.int32(16)] * 6
        for t in range(16):
            row, part, half = metas[group, 0, t], metas[group, 1, t], metas[group, 2, t]
            cls = metas[group, 3, t]
            prev = jnp.int32(16)
            for k in range(6):
                prev = jnp.where(cls == k, last[k], prev)
                last[k] = jnp.where(cls == k, t, last[k])
            pair = [sb[q, row, part, pl.ds(half * 2, 2)].reshape(128, 128) for q in range(2)]
            rows = jnp.concatenate(pair, axis=1)
            cb[t] = jnp.dot(tvb[group, t], rows, preferred_element_type=F32) + cb[prev]
        for k in range(6):
            dst, r = divmod(k, 3)
            first = pl.multiple_of((group * 3 + r) * 256, 256)
            ab[dst * 128 : (dst + 1) * 128, pl.ds(first, 256)] = cb[last[k]].astype(BF)
        return carry

    def message_out(k):
        partner(k)
        dx = QUARTERS[k]
        quarter = turn(x, dx, 4)
        cols = jnp.concatenate([wb[k, 0].reshape(3072, 128), wb[k, 1].reshape(3072, 128)], axis=1)
        part = jnp.dot(ab[...], cols, preferred_element_type=F32)
        pb[dx, 0] = part[:, 0:128].astype(BF)
        pb[dx, 1] = part[:, 128:256].astype(BF)
        for other in (1, 0):
            if dx == 0 and other == 0:
                continue
            zz = zh * 2 + (zl if other == 0 else 1 - zl)
            to = lax.rem(zz, 2)
            send(PT + dx * 2 + other, pb.at[dx, to], qb.at[dx, other], at(x_=quarter, z_=zz))

    def state_end():
        for k, step in enumerate(steps):
            got(SD + k, tiles(step, 0, 1 - c))
            got(SE + k, tiles(step, 1, 1 - c))

    send(VZP, tile(0, 0, 1), tile(0, 0, 1), dzp)
    send(VZM, tile(0, 0, 1), tile(0, 0, 1), dzm)
    weights_first(0)
    weights_first(1)
    send(SY, tile(0, 0, 0), tile(0, 0, 0), dyp)
    send(SY + 1, tile(0, 0, 0), tile(0, 0, 0), dym)
    second_y(0)
    for k in range(4):
        weight_row(zh, k)
    for k, dev in enumerate((dxp, dxm, dx2)):
        send(MET + k, metav.at[x], metav.at[x], dev)
    tv_send(0)
    got(SY, tile(0, 1, 0))
    send(SYR, y_part(ym, 0), y_part(ym, 0), dyp)
    got(SY + 1, tile(0, 2, 0))
    send(SYR + 1, y_part(yp, 1), y_part(yp, 1), dym)
    second_z(1)
    weights_far(0)
    tv_send(1)
    weights_first(2)
    second_on(0)
    state_first(0)
    second_z(2)
    weights_far(1)
    tv_send(2)
    weights_first(3)
    state_first(1)
    state_first(2)
    got(SYR, y_part(y2, 0))
    got(SYR + 1, y_part(y2, 1))
    second_z(3)
    second_on(1)
    second_on(2)
    weights_last(0)
    weights_out(0, 0)
    weights_far(2)
    state_first(3)
    state_on(1, 0)
    for d in (1, 3, 2):
        weights_out(d, 0)
    weights_last(1)
    weights_far(3)
    got(VZP + 3, half_tile(4, 0, 1, 0))
    got(VZM + 3, half_tile(4, 0, 1, 1))
    second_y(7)
    second_on(3)
    second_on(4)
    state_on(1, 1)
    state_on(1, 2)
    outs(1)
    weights_last(2)
    state_on(1, 3)
    gate_first()
    tv_send(3)
    weights_last(3)
    ons(0)
    state_on(2, 0)
    state_on(2, 1)
    second_on(5)
    second_on(6)
    outs(2)
    state_on(2, 2)
    state_on(2, 3)
    tv_on(0)
    second_on(7)
    for k in range(5):
        share(k, steps[k])
    ons(1)
    tv_on(1)
    state_on(3, 0)
    state_on(3, 1)
    outs(3)
    state_on(3, 2)
    state_on(3, 3)
    share(5, -3)
    share(6, 3)
    for n in range(8):
        second_end(n)
    ends(0)
    gate_on()
    for k in range(4):
        wb[k, :, x, :, yc] = wz[x, k]
    cb[16] = jnp.zeros((128, 256), F32)
    for k, v in enumerate((xm, xp, x2)):
        got(MET + k, metav.at[v])
    listing.start()
    ons(2)
    for j in range(4):
        got(SZP + 12 + j, half_tile(4, j, 0, 0))
        got(SZM + 12 + j, half_tile(4, j, 0, 1))
    share(7, 4)
    ends(1)
    tv_end()
    state_end()
    listing.wait()
    lax.fori_loop(0, 4, products, 0)
    ons(3)
    message_out(0)
    gate_end()
    message_out(1)
    ends(2)
    message_out(2)
    ends(3)
    message_out(3)

    hidden = sb[zl, own, y].reshape(256, 128).astype(F32)
    message = pb[0, zl].astype(F32)
    for dx in QUARTERS:
        for other in (0, 1):
            if dx == 0 and other == 0:
                continue
            got(PT + dx * 2 + other, qb.at[dx, other])
            message = message + qb[dx, other].astype(F32)
    update = jnp.tanh(message + ub_ref[...])
    gate_open = gate_ref[...]
    out_ref[...] = ((1.0 - gate_open) * hidden + gate_open * update).astype(BF)

    for d in pending:
        d.wait_send()
    for k in range(12):
        copy(WX + k, wz.at[0, 0], wb.at[0, :, 0, :, 0], dxp).wait_send()


def shards(state, rel_weight, gate_weight, gate_bias, update_bias, tile_values, tile_index, tile_count):
    src, dst, r = tile_index[0, 0], tile_index[0, 1], tile_index[0, 2]
    place = [src // 16 * 2 + (src // 2) % 2, (src // 4) % 4, src % 2]
    live = jnp.arange(16, dtype=jnp.int32) < tile_count[0, 0]
    target = jnp.where(live, dst * 3 + r, 6)
    meta = jnp.pad(jnp.stack(place + [target]), ((0, 4), (0, 112)))
    vmem = pl.BlockSpec(memory_space=pltpu.VMEM)
    hbm = pl.BlockSpec(memory_space=pl.ANY)
    return pl.pallas_call(
        kernel,
        out_shape=jax.ShapeDtypeStruct((256, 128), BF),
        in_specs=[hbm] * 7,
        out_specs=vmem,
        scratch_shapes=[
            pltpu.VMEM((1024, 128), BF),
            pltpu.VMEM((1, 128), F32),
            pltpu.VMEM((1, 128), F32),
            pltpu.VMEM((256, 128), F32),
            pltpu.VMEM((4, 16, 128, 128), BF),
            pltpu.VMEM((4, 8, 128), jnp.int32),
            pltpu.SMEM((4, 8, 128), jnp.int32),
            pltpu.VMEM((2, 8, 4, 4, 64, 128), BF),
            pltpu.VMEM((4, 2, 4, 64, 128), BF),
            pltpu.VMEM((4, 4, 2, 3, 32, 128), BF),
            pltpu.VMEM((4, 2, 4, 3, 8, 32, 128), BF),
            pltpu.VMEM((17, 128, 256), F32),
            pltpu.VMEM((256, 3072), BF),
            pltpu.VMEM((4, 2, 256, 128), BF),
            pltpu.VMEM((4, 2, 256, 128), BF),
            pltpu.SemaphoreType.DMA((S.total,)),
            pltpu.SemaphoreType.DMA((S.total,)),
            pltpu.SemaphoreType.DMA((16,)),
        ],
        compiler_params=pltpu.CompilerParams(
            collective_id=0, has_side_effects=True, vmem_limit_bytes=62 * 1024 * 1024
        ),
    )(
        meta, state.reshape(4, 64, 128), rel_weight, tile_values[0], gate_weight,
        gate_bias.reshape(1, 128), update_bias.reshape(1, 128),
    )


def solution(mesh):
    from jax.sharding import PartitionSpec as P

    in_specs = (
        P("ent", "rel"),
        P("rel", "ent", None),
        P(None, "rel"),
        P("rel"),
        P("rel"),
        P("rel", "ent", None, None),
        P("rel", None, "ent"),
        P("rel", "ent"),
    )
    return jax.shard_map(
        shards, mesh=mesh, in_specs=in_specs, out_specs=P("ent", "rel"), check_vma=False
    )
```

time: 71 us -> 68 us (0.958)
  Pallas kernels: 67.4 us -> 64.4 us
    pallas_call x1, Pallas kernels: 67.4 us -> 64.4 us  [shards(): pl.pallas_call(kernel, out_shape=jax.ShapeDtypeStruct((256, 128), BF), in...]
where the time goes in v3:
time: 68 us; the launch traced here: 67.9 us
  Pallas kernels  64.4 us (95%)
  local copies, waits for them, and re-layouts  2.75 us (4%)
  between operations  0.68 us (1%)
    pallas_call x1, Pallas kernels, shards(): pl.pallas_call(kernel, out_shape=jax.ShapeDtypeStruct((256, 128), BF), in...  64.4 us
    unnamed x3, local copies, waits for them, and re-layouts  2.15 us

profile of v3, /device:TPU:1, one launch (start us, length us, event | category | flops | bytes accessed | tf_op | source)
XLA Modules:
  0.0 67.9 jit_solution(9775096114822122995)
XLA Ops:
  0.7 0.0 copy-start
  0.7 0.7 copy-done
  1.4 0.6 pad.4.meta_in
  2.0 64.4 %shard_map.82 = bf16[256,128]{1,0:T(8,128)(2,1)} custom-call(s32[8,128]{1,0:T(8,128)} %pad.4.meta_in, bf16[4,64,128]{2,1,0:T(8,128)(2,1)} %bitcast.34, bf16[3,32,1024]{2,1,0:T(8,128)(2,1)} %relw_in.1, bf16[16,128,128]{2,1,0:T(8,128)(2,1)} %bitcast.33, bf16[1024,128]{1,0:T(8,128)(2,1)} %gw_in.1, f32[1,128]{1,0:T(1,128)} %bitcast.35, f32[1,128]{1,0:T(1,128)} %bitcast.36), custom_call_target="tpu_custom_call" | custom-call | tf_op jit(solution)/shard_map/pallas_call | solution.py:488
  66.4 1.5 %copy.11 = bf16[256,128]{1,0:T(8,128)(2,1)} copy(bf16[256,128]{1,0:T(8,128)(2,1)} %shard_map.82) | data formatting | bytes 131072
  (3 shorter events, 0.0 us)
Async XLA Ops:
  0.7 0.7 %copy-start = (s32[1,3,16]{2,0,1:T(1,128)S(1)}, s32[1,3,16]{2,0,1:T(1,128)}, u32[]{:S(2)}) copy-start(s32[1,3,16]{2,0,1:T(1,128)} %param.14) | copy-start | bytes 580
